TPU v7x, 256 devices: a whole 4x4x8 slice. The times are simulated.
256 devices in a mesh: blk: 128 (over y, z, x_hi, core), mp: 2 (over x_lo).
Axes of the slice: x: 4 (x_hi: 2, x_lo: 2; x = x_hi * 2 + x_lo), y: 4, z: 8, core: 2. Of those that a mesh axis runs over, the one named last changes fastest.
Arguments:
- params: bfloat16 [128, 1024, 4096], P('blk', None, 'mp'), may hold values from -0.09375 to 0.09375
- hidden: bfloat16 [128, 384, 4096], P('blk', None, 'mp'), may hold values from -6 to 6
- targets: bfloat16 [128, 384, 1024], P('blk', None, 'mp'), may hold values from -6 to 6
Outputs:
- params_out: bfloat16 [128, 1024, 4096], P('blk', None, 'mp')
- errors: float32 [2], replicated
All inputs are finite; a program needn't handle non-finite values.
Results may differ from a plain program's by a relative error of at most 0.0085.
Values may be sent and summed in bfloat16 or wider, within the bound.
A program may use at most 128 MiB of HBM per device.

v0:
```python
import functools
import jax
import jax.numpy as jnp
from jax import lax
from jax.sharding import Mesh
from jax.sharding import PartitionSpec as P

ITERS = 2
BLK = ("blk_0", "blk_1", "blk_2", "blk_3")
BLK_MP = ("blk_0", "blk_1", "blk_2", "blk_3", "mp")
mix_third = 1.0 / 3.0
step_size = 0.1


def from_behind(block, axis, distance):
    devices = range(lax.axis_size(axis))
    route = [((i - distance) % len(devices), i) for i in devices]
    return lax.ppermute(block, axis, route)


def from_everyone(x, axis):
    copies = jnp.broadcast_to(x, (lax.axis_size(axis), *x.shape))
    return lax.all_to_all(copies, axis, split_axis=0, concat_axis=0, tiled=True)


def taken_together(x, axis):
    return from_everyone(x, axis).sum(axis=0)


def over_axes(x, axes):
    return functools.reduce(lax.psum, axes, x)


def send_tracker(track):
    track_left = from_behind(track, BLK, 1)
    track_right = from_behind(track, BLK, -1)
    return (track_left, track_right)


def on_device(params, hidden, targets):
    state = params[0]
    feats = hidden[0]
    targ_local = targets[0]
    tokens = feats.shape[0]
    hidden_total = state.shape[1] * lax.axis_size("mp")
    replicas = lax.axis_size(BLK)
    full_targ = lax.all_gather(targ_local, "mp", axis=1, tiled=True)

    def gradient(weight):
        partial_value = lax.dot_general(
            feats, weight, (((1,), (1,)), ((), ())), preferred_element_type=jnp.float32
        )
        output = taken_together(partial_value, "mp")
        resid = (output - full_targ.astype(jnp.float32)).astype(jnp.bfloat16)
        grad = lax.dot_general(
            resid, feats, (((0,), (0,)), ((), ())), preferred_element_type=jnp.float32
        )
        return grad / tokens

    older = gradient(state)
    fresh = older
    track = older.astype(jnp.bfloat16)
    track_left, track_right = send_tracker(track)
    err_list = []
    for step in range(ITERS):
        state_left = from_behind(state, BLK, 1)
        state_right = from_behind(state, BLK, -1)
        if step > 0:
            track_mix = (
                track_left.astype(jnp.float32)
                + track.astype(jnp.float32)
                + track_right.astype(jnp.float32)
            ) * mix_third
            track = (track_mix + fresh - older).astype(jnp.bfloat16)
            older = fresh
        own_state = state.astype(jnp.float32)
        diff = own_state - state_right.astype(jnp.float32)
        local_err = jnp.sum(diff * diff) / (hidden_total * replicas)
        err_list.append(local_err)
        blended = (
            state_left.astype(jnp.float32) + own_state + state_right.astype(jnp.float32)
        ) * mix_third
        new_state = (blended - step_size * track.astype(jnp.float32)).astype(jnp.bfloat16)
        if step < ITERS - 1:
            fresh = gradient(new_state)
        state = new_state
    errors = jnp.stack(err_list)
    errors = over_axes(errors, BLK_MP)
    return (state[None], errors)


def solution(mesh):
    torus = Mesh(
        mesh.devices.reshape(4, 8, 2, 2, mesh.shape["mp"]),
        ("blk_0", "blk_1", "blk_2", "blk_3", "mp"),
    )
    placed = (P(BLK, None, "mp"), P(BLK, None, "mp"), P(BLK, None, "mp"))
    return jax.shard_map(
        on_device, mesh=torus, in_specs=placed, out_specs=(P(BLK, None, "mp"), P()), check_vma=False
    )
```

profile of v0, /device:TPU:194, one launch (start us, length us, event | category | flops | bytes accessed | tf_op | source)
XLA Modules:
  0.0 420.3 jit_solution(9891182136154639013)
XLA Ops:
  0.6 0.0 copy-start
  0.6 2.1 collective-permute-start.1
  2.7 0.0 collective-permute-start
  2.7 0.0 copy-done
  2.7 4.0 fusion.23
  6.8 2.1 broadcast_in_dim.9
  8.8 0.0 copy-start.2
  8.8 6.8 %all-to-all-start = ((f32[2,384,1024]{2,1,0:T(8,128)}), f32[2,384,1024]{2,1,0:T(8,128)}, u32[]{:S(2)}, u32[]{:S(2)}) async-start(f32[2,384,1024]{2,1,0:T(8,128)} %broadcast_in_dim.9), calls=%async_computation | async-start | bytes 6291456 | tf_op jit(solution)/shard_map/all_to_all | solution.py:23
  15.6 0.0 copy-done.2
  15.6 78.1 %all-gather = bf16[1,384,1024]{2,1,0:T(8,128)(2,1)} all-gather(bf16[1,384,512]{2,1,0:T(8,128)(2,1)S(1)} %copy-done.2), channel_id=2, replica_groups=mesh['blk_0'=4,'blk_1'=8,'blk_2'=2,'blk_3'=2,'mp'=2] {'mp'}, dimensions={2}, use_global_device_ids=true | all-gather | bytes 1179648 | tf_op jit(solution)/shard_map/all_gather | solution.py:47
  93.6 0.0 all-to-all-done
  93.6 2.3 reduce_sum.36
  96.0 0.0 collective-permute-done.1
  96.0 0.0 collective-permute-done
  96.0 13.7 %fusion.4 = (f32[]{:T(128)}, bf16[1024,2048]{1,0:T(8,128)(2,1)}, bf16[1024,2048]{1,0:T(8,128)(2,1)}, f32[1024,2048]{1,0:T(8,128)}) fusion(bf16[1024,2048]{1,0:T(8,128)(2,1)} %collective-permute-done.1, bf16[1,1024,2048]{2,1,0:T(8,128)(2,1)} %param.3, bf16[1024,2048]{1,0:T(8,128)(2,1)} %collective-permute-done, bf16[1,384,2048]{2,1,0:T(8,128)(2,1)S(1)} %copy-done, ...), kind=kOutput, calls=%fused_computation.12 | convolution fusion | flops 1643249664 | bytes 33292292 | tf_op jit(solution)/shard_map/dot_general | solution.py:55
  109.7 3.0 collective-permute-start.3
  112.7 86.1 %collective-permute-start.4 = (bf16[1024,2048]{1,0:T(8,128)(2,1)}, bf16[1024,2048]{1,0:T(8,128)(2,1)}, u32[]{:S(2)}, u32[]{:S(2)}) collective-permute-start(bf16[1024,2048]{1,0:T(8,128)(2,1)} %get-tuple-element.4), channel_id=1, source_target_pairs={{254,0},{0,2},{2,4},{4,6},{6,8},{8,10},{10,12},{12,14},{14,16},{16... | collective-permute-start | bytes 12582920 | tf_op jit(solution)/shard_map/ppermute | solution.py:18
  198.8 0.0 collective-permute-start.5
  198.8 3.2 collective-permute-start.2
  202.1 4.0 fusion.25
  206.1 2.1 broadcast_in_dim.10
  208.2 6.6 %all-to-all-start.1 = ((f32[2,384,1024]{2,1,0:T(8,128)}), f32[2,384,1024]{2,1,0:T(8,128)}, u32[]{:S(2)}, u32[]{:S(2)}) async-start(f32[2,384,1024]{2,1,0:T(8,128)} %broadcast_in_dim.10), calls=%async_computation.1 | async-start | bytes 6291456 | tf_op jit(solution)/shard_map/all_to_all | solution.py:23
  215.4 0.0 collective-permute-done.3
  215.4 6.3 %fusion.14 = f32[]{:T(128)} fusion(bf16[1024,2048]{1,0:T(8,128)(2,1)} %collective-permute-done.3, bf16[1024,2048]{1,0:T(8,128)(2,1)} %get-tuple-element.3), kind=kLoop, calls=%fused_computation.22 | loop fusion | flops 10485759 | bytes 8388612 | tf_op jit(solution)/shard_map/reduce_sum | solution.py:78
  221.7 0.0 copy-start.1
  222.4 0.1 pad_maximum_fusion
  222.5 10.7 %psum.35 = f32[2]{0:T(128)S(1)} all-reduce(f32[2]{0:T(128)S(1)} %pad_maximum_fusion), channel_id=1, replica_groups=mesh['blk_0'=4,'blk_1'=8,'blk_2'=2,'blk_3'=2,'mp'=2] {'blk_0'}, use_global_device_ids=true, to_apply=%region_4.0 | all-reduce | flops 2 | bytes 16 | tf_op jit(solution)/shard_map/psum | solution.py:31
  233.2 22.5 %psum.36 = f32[2]{0:T(128)S(1)} all-reduce(f32[2]{0:T(128)S(1)} %psum.35), channel_id=1, replica_groups=mesh['blk_0'=4,'blk_1'=8,'blk_2'=2,'blk_3'=2,'mp'=2] {'blk_1'}, use_global_device_ids=true, to_apply=%region_5.0 | all-reduce | flops 2 | bytes 16 | tf_op jit(solution)/shard_map/psum | solution.py:31
  255.7 138.1 %psum.37 = f32[2]{0:T(128)S(1)} all-reduce(f32[2]{0:T(128)S(1)} %psum.36), channel_id=1, replica_groups=mesh['blk_0'=4,'blk_1'=8,'blk_2'=2,'blk_3'=2,'mp'=2] {'blk_2'}, use_global_device_ids=true, to_apply=%region_6.0 | all-reduce | flops 2 | bytes 16 | tf_op jit(solution)/shard_map/psum | solution.py:31
  393.7 2.4 psum.38
  396.2 0.0 all-to-all-done.1
  396.2 3.5 reduce_sum.37
  399.6 5.4 %psum.39 = f32[2]{0:T(128)} all-reduce(f32[2]{0:T(128)S(1)} %psum.38), channel_id=1, replica_groups=mesh['blk_0'=4,'blk_1'=8,'blk_2'=2,'blk_3'=2,'mp'=2] {'mp'}, use_global_device_ids=true, to_apply=%region_8.0 | all-reduce | flops 2 | bytes 16 | tf_op jit(solution)/shard_map/psum | solution.py:31
  405.1 0.0 collective-permute-done.4
  405.1 0.0 collective-permute-done.5
  405.1 0.0 collective-permute-done.2
  405.1 0.0 copy-done.1
  405.1 15.3 %fusion.15 = bf16[1,1024,2048]{2,1,0:T(8,128)(2,1)} fusion(bf16[1024,2048]{1,0:T(8,128)(2,1)} %collective-permute-done.3, bf16[1024,2048]{1,0:T(8,128)(2,1)} %get-tuple-element.3, bf16[1024,2048]{1,0:T(8,128)(2,1)} %collective-permute-done.2, f32[1024,2048]{1,0:T(8,128)} %get-tuple-element.5, bf16[1024,2048]{1,0:T(8,128)(2,1)} %collective-permute-done.5, ...), kind=kOutput, calls=%fused_computation.24 | convolution fusion | flops 1657929728 | bytes 37486592 | tf_op jit(solution)/shard_map/dot_general | solution.py:55
Async XLA Ops:
  0.6 2.1 copy-start
  0.6 95.3 %collective-permute-start.1 = (bf16[1024,2048]{1,0:T(8,128)(2,1)}, bf16[1024,2048]{1,0:T(8,128)(2,1)}, u32[]{:S(2)}, u32[]{:S(2)}) collective-permute-start(bf16[1024,2048]{1,0:T(8,128)(2,1)} %bitcast.37), channel_id=1, source_target_pairs={{2,0},{4,2},{6,4},{8,6},{10,8},{12,10},{14,12},{16,14},{18,16},{20... | collective-permute-start | bytes 12582920 | tf_op jit(solution)/shard_map/ppermute | solution.py:18
  2.7 93.2 %collective-permute-start = (bf16[1024,2048]{1,0:T(8,128)(2,1)}, bf16[1024,2048]{1,0:T(8,128)(2,1)}, u32[]{:S(2)}, u32[]{:S(2)}) collective-permute-start(bf16[1024,2048]{1,0:T(8,128)(2,1)} %bitcast.38), channel_id=1, source_target_pairs={{254,0},{0,2},{2,4},{4,6},{6,8},{8,10},{10,12},{12,14},{14,16},{16... | collective-permute-start | bytes 12582920 | tf_op jit(solution)/shard_map/ppermute | solution.py:18
  8.8 6.8 %copy-start.2 = (bf16[1,384,512]{2,1,0:T(8,128)(2,1)S(1)}, bf16[1,384,512]{2,1,0:T(8,128)(2,1)}, u32[]{:S(2)}) copy-start(bf16[1,384,512]{2,1,0:T(8,128)(2,1)} %param.5) | copy-start | bytes 1179652
  8.8 84.8 %all-to-all-start = ((f32[2,384,1024]{2,1,0:T(8,128)}), f32[2,384,1024]{2,1,0:T(8,128)}, u32[]{:S(2)}, u32[]{:S(2)}) async-start(f32[2,384,1024]{2,1,0:T(8,128)} %broadcast_in_dim.9), calls=%async_computation | async-start | bytes 6291456 | tf_op jit(solution)/shard_map/all_to_all | solution.py:23
  109.7 105.7 %collective-permute-start.3 = (bf16[1024,2048]{1,0:T(8,128)(2,1)}, bf16[1024,2048]{1,0:T(8,128)(2,1)}, u32[]{:S(2)}, u32[]{:S(2)}) collective-permute-start(bf16[1024,2048]{1,0:T(8,128)(2,1)} %get-tuple-element.3), channel_id=1, source_target_pairs={{2,0},{4,2},{6,4},{8,6},{10,8},{12,10},{14,12},{16,14},{18,16},{20... | collective-permute-start | bytes 12582920 | tf_op jit(solution)/shard_map/ppermute | solution.py:18
  112.7 292.4 %collective-permute-start.4 = (bf16[1024,2048]{1,0:T(8,128)(2,1)}, bf16[1024,2048]{1,0:T(8,128)(2,1)}, u32[]{:S(2)}, u32[]{:S(2)}) collective-permute-start(bf16[1024,2048]{1,0:T(8,128)(2,1)} %get-tuple-element.4), channel_id=1, source_target_pairs={{254,0},{0,2},{2,4},{4,6},{6,8},{8,10},{10,12},{12,14},{14,16},{16... | collective-permute-start | bytes 12582920 | tf_op jit(solution)/shard_map/ppermute | solution.py:18
  198.8 206.2 %collective-permute-start.5 = (bf16[1024,2048]{1,0:T(8,128)(2,1)}, bf16[1024,2048]{1,0:T(8,128)(2,1)}, u32[]{:S(2)}, u32[]{:S(2)}) collective-permute-start(bf16[1024,2048]{1,0:T(8,128)(2,1)} %get-tuple-element.4), channel_id=1, source_target_pairs={{2,0},{4,2},{6,4},{8,6},{10,8},{12,10},{14,12},{16,14},{18,16},{20... | collective-permute-start | bytes 12582920 | tf_op jit(solution)/shard_map/ppermute | solution.py:18
  198.8 206.2 %collective-permute-start.2 = (bf16[1024,2048]{1,0:T(8,128)(2,1)}, bf16[1024,2048]{1,0:T(8,128)(2,1)}, u32[]{:S(2)}, u32[]{:S(2)}) collective-permute-start(bf16[1024,2048]{1,0:T(8,128)(2,1)} %get-tuple-element.3), channel_id=1, source_target_pairs={{254,0},{0,2},{2,4},{4,6},{6,8},{8,10},{10,12},{12,14},{14,16},{16... | collective-permute-start | bytes 12582920 | tf_op jit(solution)/shard_map/ppermute | solution.py:18
  208.2 188.0 %all-to-all-start.1 = ((f32[2,384,1024]{2,1,0:T(8,128)}), f32[2,384,1024]{2,1,0:T(8,128)}, u32[]{:S(2)}, u32[]{:S(2)}) async-start(f32[2,384,1024]{2,1,0:T(8,128)} %broadcast_in_dim.10), calls=%async_computation.1 | async-start | bytes 6291456 | tf_op jit(solution)/shard_map/all_to_all | solution.py:23
  221.7 183.4 %copy-start.1 = (bf16[1,384,1024]{2,1,0:T(8,128)(2,1)S(1)}, bf16[1,384,1024]{2,1,0:T(8,128)(2,1)}, u32[]{:S(2)}) copy-start(bf16[1,384,1024]{2,1,0:T(8,128)(2,1)} %all-gather) | copy-start | bytes 2359300
where the time goes:
time: 421 us; the launch traced here: 420 us
  blocking collectives  257 us (61%)
  starting transfers between devices  108 us (26%)
  matrix products  37.1 us (9%)
  other arithmetic  12.1 us (3%)
    psum x5, blocking collectives, over_axes(): return functools.reduce(lax.psum, axes, x)  179 us
    ppermute x6, starting transfers between devices, from_behind(): return lax.ppermute(block, axis, route)  94.4 us
    all_gather x1, blocking collectives, on_device(): full_targ = lax.all_gather(targ_local, 'mp', axis=1, tiled=True)  78.1 us
    dot_general x2, matrix products, gradient(): lax.dot_general(resid, feats, (((0,), (0,)), ((), ())), preferred_element...  29 us
    all_to_all x2, starting transfers between devices, from_everyone(): return lax.all_to_all(copies, axis, split_axis=0, concat_axis=0, tiled=True)  13.3 us
  transfers between devices with their start and end apart: 8, of which 0 were waited for; matrix products, arithmetic and copies ran while one was open for 6% of the time, Pallas kernels for 0%

commit v1 on v0

--- a/solution.py
+++ b/solution.py
@@ -44,7 +44,7 @@
     tokens = feats.shape[0]
     hidden_total = state.shape[1] * lax.axis_size("mp")
     replicas = lax.axis_size(BLK)
-    full_targ = lax.all_gather(targ_local, "mp", axis=1, tiled=True)
+    full_targ = jnp.concatenate(lax.all_gather(targ_local, "mp"), axis=1)
 
     def gradient(weight):
         partial_value = lax.dot_general(

time: 421 us -> 416 us (0.988); the launches traced: 420 us -> 411 us
  blocking collectives: 257 us -> 208 us
  waiting for transfers between devices: 0.02 us -> 25.6 us
  local copies, waits for them, and re-layouts: 4.16 us -> 15.1 us
  other arithmetic: 12.1 us -> 16.4 us
    psum x5, blocking collectives: 179 us -> 130 us  [over_axes(): return functools.reduce(lax.psum, axes, x)]
    all_to_all x2, waiting for transfers between devices: 0.01 us -> 25.6 us  [from_everyone(): return lax.all_to_all(copies, axis, split_axis=0, concat_axis=0, tiled=True)]
    reduce_sum x0 -> x2, local copies, waits for them, and re-layouts: none -> 6.1 us  [taken_together(): return from_everyone(x, axis).sum(axis=0)]
  transfers between devices with their start and end apart: 8 -> 8, of which waited for: 0 -> 1; matrix products, arithmetic and copies ran while one was open for 6% -> 10% of each run, Pallas kernels for 0% -> 0%
where the time goes in v1:
time: 416 us; the launch traced here: 411 us
  blocking collectives  208 us (50%)
  starting transfers between devices  108 us (26%)
  matrix products  36.1 us (9%)
  waiting for transfers between devices  25.6 us (6%)
  other arithmetic  16.4 us (4%)
  local copies, waits for them, and re-layouts  15.1 us (4%)
    psum x5, blocking collectives, over_axes(): return functools.reduce(lax.psum, axes, x)  130 us
    ppermute x6, starting transfers between devices, from_behind(): return lax.ppermute(block, axis, route)  94.5 us
    all_gather x1, blocking collectives, on_device(): full_targ = jnp.concatenate(lax.all_gather(targ_local, 'mp'), axis=1)  77.9 us
    dot_general x2, matrix products, gradient(): lax.dot_general(resid, feats, (((0,), (0,)), ((), ())), preferred_element...  26.4 us
    all_to_all x2, waiting for transfers between devices, from_everyone(): return lax.all_to_all(copies, axis, split_axis=0, concat_axis=0, tiled=True)  25.6 us
    all_to_all x2, starting transfers between devices, from_everyone(): return lax.all_to_all(copies, axis, split_axis=0, concat_axis=0, tiled=True)  13.3 us
    dot_general x2, matrix products, gradient(): lax.dot_general(feats, weight, (((1,), (1,)), ((), ())), preferred_elemen...  9.7 us
  transfers between devices with their start and end apart: 8, of which 1 were waited for; matrix products, arithmetic and copies ran while one was open for 10% of the time, Pallas kernels for 0%

profile of v1, /device:TPU:194, one launch (start us, length us, event | category | flops | bytes accessed | tf_op | source)
XLA Modules:
  0.0 410.7 jit_solution(1578110732319820831)
XLA Ops:
  0.6 0.0 copy-start
  0.6 2.1 collective-permute-start.1
  2.7 0.0 collective-permute-start
  2.7 0.0 copy-done
  2.7 4.0 fusion.23
  6.8 2.1 broadcast_in_dim.9
  8.8 0.0 copy-start.1
  8.8 6.8 %all-to-all-start = ((f32[2,384,1024]{2,1,0:T(8,128)}), f32[2,384,1024]{2,1,0:T(8,128)}, u32[]{:S(2)}, u32[]{:S(2)}) async-start(f32[2,384,1024]{2,1,0:T(8,128)} %broadcast_in_dim.9), calls=%async_computation | async-start | bytes 6291456 | tf_op jit(solution)/shard_map/all_to_all | solution.py:23
  15.6 0.0 copy-done.1
  15.6 77.9 %all_gather.3 = bf16[2,384,512]{2,1,0:T(8,128)(2,1)S(1)} all-gather(bf16[1,384,512]{2,1,0:T(8,128)(2,1)S(1)} %copy-done.1), channel_id=1, replica_groups=mesh['blk_0'=4,'blk_1'=8,'blk_2'=2,'blk_3'=2,'mp'=2] {'mp'}, dimensions={0}, use_global_device_ids=true | all-gather | bytes 1179648 | tf_op jit(solution)/shard_map/all_gather | solution.py:47
  93.5 0.4 copy.11
  93.9 0.0 all-to-all-done
  93.9 3.5 reduce_sum.40
  97.4 3.0 copy.10
  100.4 1.6 fusion.16
  102.0 0.0 collective-permute-done.1
  102.0 0.0 collective-permute-done
  102.0 12.1 %fusion.4 = (f32[]{:T(128)}, bf16[1024,2048]{1,0:T(8,128)(2,1)}, bf16[1024,2048]{1,0:T(8,128)(2,1)}, f32[1024,2048]{1,0:T(8,128)}) fusion(bf16[1024,2048]{1,0:T(8,128)(2,1)} %collective-permute-done.1, bf16[1,1024,2048]{2,1,0:T(8,128)(2,1)} %param.3, bf16[1024,2048]{1,0:T(8,128)(2,1)} %collective-permute-done, bf16[384,1024]{0,1:T(8,128)(2,1)S(1)} %bitcast.42, ...), kind=kOutput, calls=%fused_computation.12 | convolution fusion | flops 1642070016 | bytes 31719428 | tf_op jit(solution)/shard_map/dot_general | solution.py:55
  114.1 3.1 collective-permute-start.3
  117.2 86.1 %collective-permute-start.4 = (bf16[1024,2048]{1,0:T(8,128)(2,1)}, bf16[1024,2048]{1,0:T(8,128)(2,1)}, u32[]{:S(2)}, u32[]{:S(2)}) collective-permute-start(bf16[1024,2048]{1,0:T(8,128)(2,1)} %get-tuple-element.4), channel_id=1, source_target_pairs={{254,0},{0,2},{2,4},{4,6},{6,8},{8,10},{10,12},{12,14},{14,16},{16... | collective-permute-start | bytes 12582920 | tf_op jit(solution)/shard_map/ppermute | solution.py:18
  203.3 0.0 collective-permute-start.5
  203.3 3.2 collective-permute-start.2
  206.5 5.7 %fusion.25 = f32[384,1024]{0,1:T(8,128)} fusion(bf16[1024,2048]{1,0:T(8,128)(2,1)} %get-tuple-element.3, bf16[1,384,2048]{2,1,0:T(8,128)(2,1)S(1)} %copy-done), kind=kOutput, calls=%fused_computation.36 | convolution fusion | flops 1610612736 | bytes 7340032 | tf_op jit(solution)/shard_map/dot_general | solution.py:50
  212.2 3.1 copy.12
  215.3 3.5 broadcast_in_dim.10
  218.8 6.6 %all-to-all-start.1 = ((f32[2,384,1024]{2,1,0:T(8,128)}), f32[2,384,1024]{2,1,0:T(8,128)}, u32[]{:S(2)}, u32[]{:S(2)}) async-start(f32[2,384,1024]{2,1,0:T(8,128)} %broadcast_in_dim.10), calls=%async_computation.1 | async-start | bytes 6291456 | tf_op jit(solution)/shard_map/all_to_all | solution.py:23
  226.0 0.0 collective-permute-done.3
  226.0 6.3 %fusion.14 = f32[]{:T(128)} fusion(bf16[1024,2048]{1,0:T(8,128)(2,1)} %collective-permute-done.3, bf16[1024,2048]{1,0:T(8,128)(2,1)} %get-tuple-element.3), kind=kLoop, calls=%fused_computation.22 | loop fusion | flops 10485759 | bytes 8388612 | tf_op jit(solution)/shard_map/reduce_sum | solution.py:78
  232.9 0.1 pad_maximum_fusion
  233.0 10.7 %psum.35 = f32[2]{0:T(128)S(1)} all-reduce(f32[2]{0:T(128)S(1)} %pad_maximum_fusion), channel_id=1, replica_groups=mesh['blk_0'=4,'blk_1'=8,'blk_2'=2,'blk_3'=2,'mp'=2] {'blk_0'}, use_global_device_ids=true, to_apply=%region_4.0 | all-reduce | flops 2 | bytes 16 | tf_op jit(solution)/shard_map/psum | solution.py:31
  243.7 16.4 %psum.36 = f32[2]{0:T(128)S(1)} all-reduce(f32[2]{0:T(128)S(1)} %psum.35), channel_id=1, replica_groups=mesh['blk_0'=4,'blk_1'=8,'blk_2'=2,'blk_3'=2,'mp'=2] {'blk_1'}, use_global_device_ids=true, to_apply=%region_5.0 | all-reduce | flops 2 | bytes 16 | tf_op jit(solution)/shard_map/psum | solution.py:31
  260.1 25.6 %all-to-all-done.1 = f32[2,384,1024]{2,1,0:T(8,128)} async-done(((f32[2,384,1024]{2,1,0:T(8,128)}), f32[2,384,1024]{2,1,0:T(8,128)}, u32[]{:S(2)}, u32[]{:S(2)}) %all-to-all-start.1) | async-done | bytes 3145760 | tf_op jit(solution)/shard_map/all_to_all | solution.py:23
  285.7 3.5 reduce_sum.42
  289.1 94.7 %psum.37 = f32[2]{0:T(128)S(1)} all-reduce(f32[2]{0:T(128)S(1)} %psum.36), channel_id=1, replica_groups=mesh['blk_0'=4,'blk_1'=8,'blk_2'=2,'blk_3'=2,'mp'=2] {'blk_2'}, use_global_device_ids=true, to_apply=%region_6.0 | all-reduce | flops 2 | bytes 16 | tf_op jit(solution)/shard_map/psum | solution.py:31
  383.9 3.1 copy.13
  387.0 2.4 psum.38
  389.4 1.6 fusion.17
  391.0 5.4 %psum.39 = f32[2]{0:T(128)} all-reduce(f32[2]{0:T(128)S(1)} %psum.38), channel_id=1, replica_groups=mesh['blk_0'=4,'blk_1'=8,'blk_2'=2,'blk_3'=2,'mp'=2] {'mp'}, use_global_device_ids=true, to_apply=%region_8.0 | all-reduce | flops 2 | bytes 16 | tf_op jit(solution)/shard_map/psum | solution.py:31
  396.4 0.0 collective-permute-done.4
  396.4 0.0 collective-permute-done.5
  396.4 0.0 collective-permute-done.2
  396.4 14.3 %fusion.15 = bf16[1,1024,2048]{2,1,0:T(8,128)(2,1)} fusion(bf16[1024,2048]{1,0:T(8,128)(2,1)} %collective-permute-done.3, bf16[1024,2048]{1,0:T(8,128)(2,1)} %get-tuple-element.3, bf16[1024,2048]{1,0:T(8,128)(2,1)} %collective-permute-done.2, f32[1024,2048]{1,0:T(8,128)} %get-tuple-element.5, bf16[384,1024]{0,1:T(8,128)(2,1)S(1)} %bitcast.43, ...), kind=kOutput, calls=%fused_computation.24 | convolution fusion | flops 1656750080 | bytes 35913728 | tf_op jit(solution)/shard_map/dot_general | solution.py:55
Async XLA Ops:
  0.6 2.1 copy-start
  0.6 101.3 %collective-permute-start.1 = (bf16[1024,2048]{1,0:T(8,128)(2,1)}, bf16[1024,2048]{1,0:T(8,128)(2,1)}, u32[]{:S(2)}, u32[]{:S(2)}) collective-permute-start(bf16[1024,2048]{1,0:T(8,128)(2,1)} %bitcast.40), channel_id=1, source_target_pairs={{2,0},{4,2},{6,4},{8,6},{10,8},{12,10},{14,12},{16,14},{18,16},{20... | collective-permute-start | bytes 12582920 | tf_op jit(solution)/shard_map/ppermute | solution.py:18
  2.7 99.2 %collective-permute-start = (bf16[1024,2048]{1,0:T(8,128)(2,1)}, bf16[1024,2048]{1,0:T(8,128)(2,1)}, u32[]{:S(2)}, u32[]{:S(2)}) collective-permute-start(bf16[1024,2048]{1,0:T(8,128)(2,1)} %bitcast.41), channel_id=1, source_target_pairs={{254,0},{0,2},{2,4},{4,6},{6,8},{8,10},{10,12},{12,14},{14,16},{16... | collective-permute-start | bytes 12582920 | tf_op jit(solution)/shard_map/ppermute | solution.py:18
  8.8 6.8 %copy-start.1 = (bf16[1,384,512]{2,1,0:T(8,128)(2,1)S(1)}, bf16[1,384,512]{2,1,0:T(8,128)(2,1)}, u32[]{:S(2)}) copy-start(bf16[1,384,512]{2,1,0:T(8,128)(2,1)} %param.5) | copy-start | bytes 1179652
  8.8 85.1 %all-to-all-start = ((f32[2,384,1024]{2,1,0:T(8,128)}), f32[2,384,1024]{2,1,0:T(8,128)}, u32[]{:S(2)}, u32[]{:S(2)}) async-start(f32[2,384,1024]{2,1,0:T(8,128)} %broadcast_in_dim.9), calls=%async_computation | async-start | bytes 6291456 | tf_op jit(solution)/shard_map/all_to_all | solution.py:23
  114.1 111.9 %collective-permute-start.3 = (bf16[1024,2048]{1,0:T(8,128)(2,1)}, bf16[1024,2048]{1,0:T(8,128)(2,1)}, u32[]{:S(2)}, u32[]{:S(2)}) collective-permute-start(bf16[1024,2048]{1,0:T(8,128)(2,1)} %get-tuple-element.3), channel_id=1, source_target_pairs={{2,0},{4,2},{6,4},{8,6},{10,8},{12,10},{14,12},{16,14},{18,16},{20... | collective-permute-start | bytes 12582920 | tf_op jit(solution)/shard_map/ppermute | solution.py:18
  117.2 279.3 %collective-permute-start.4 = (bf16[1024,2048]{1,0:T(8,128)(2,1)}, bf16[1024,2048]{1,0:T(8,128)(2,1)}, u32[]{:S(2)}, u32[]{:S(2)}) collective-permute-start(bf16[1024,2048]{1,0:T(8,128)(2,1)} %get-tuple-element.4), channel_id=1, source_target_pairs={{254,0},{0,2},{2,4},{4,6},{6,8},{8,10},{10,12},{12,14},{14,16},{16... | collective-permute-start | bytes 12582920 | tf_op jit(solution)/shard_map/ppermute | solution.py:18
  203.3 193.1 %collective-permute-start.5 = (bf16[1024,2048]{1,0:T(8,128)(2,1)}, bf16[1024,2048]{1,0:T(8,128)(2,1)}, u32[]{:S(2)}, u32[]{:S(2)}) collective-permute-start(bf16[1024,2048]{1,0:T(8,128)(2,1)} %get-tuple-element.4), channel_id=1, source_target_pairs={{2,0},{4,2},{6,4},{8,6},{10,8},{12,10},{14,12},{16,14},{18,16},{20... | collective-permute-start | bytes 12582920 | tf_op jit(solution)/shard_map/ppermute | solution.py:18
  203.3 193.1 %collective-permute-start.2 = (bf16[1024,2048]{1,0:T(8,128)(2,1)}, bf16[1024,2048]{1,0:T(8,128)(2,1)}, u32[]{:S(2)}, u32[]{:S(2)}) collective-permute-start(bf16[1024,2048]{1,0:T(8,128)(2,1)} %get-tuple-element.3), channel_id=1, source_target_pairs={{254,0},{0,2},{2,4},{4,6},{6,8},{8,10},{10,12},{12,14},{14,16},{16... | collective-permute-start | bytes 12582920 | tf_op jit(solution)/shard_map/ppermute | solution.py:18
  218.8 66.9 %all-to-all-start.1 = ((f32[2,384,1024]{2,1,0:T(8,128)}), f32[2,384,1024]{2,1,0:T(8,128)}, u32[]{:S(2)}, u32[]{:S(2)}) async-start(f32[2,384,1024]{2,1,0:T(8,128)} %broadcast_in_dim.10), calls=%async_computation.1 | async-start | bytes 6291456 | tf_op jit(solution)/shard_map/all_to_all | solution.py:23
